TPU v7x, 256 devices: a whole 4x4x8 slice. The times are simulated.
256 devices in a mesh: dp: 8 (over x, core), expert: 32 (over y, z).
Axes of the slice: x: 4, y: 4, z: 8, core: 2. Of those that a mesh axis runs over, the one named last changes fastest.
Arguments:
- queries: bfloat16 [2048, 16, 3072], P('expert', 'dp'), may hold values from -256 to 256
- key_nope: bfloat16 [2048, 16, 2048], P('expert', 'dp'), may hold values from -4 to 4
- key_rope: bfloat16 [2048, 16, 64], P('expert', 'dp'), may hold values from -4 to 4
- values: bfloat16 [2048, 16, 2048], P('expert', 'dp'), may hold values from -6 to 6
- residual: bfloat16 [2048, 16, 2048], P('expert', 'dp'), may hold values from -6 to 6
- segments: int32 [16, 2048], P('dp'), may hold values from 0 to 1, never falling along the last dimension, each value on 1 to 1536 neighbouring positions
- out_proj: bfloat16 [2048, 2048], P(('dp', 'expert')), may hold values from -0.125 to 0.125
- norm_gain: bfloat16 [2048], replicated, may hold values from 0.5 to 1.5
- expert_gate: bfloat16 [32, 2048, 704], P('expert'), may hold values from -0.125 to 0.125
- expert_up: bfloat16 [32, 2048, 704], P('expert'), may hold values from -0.125 to 0.125
- expert_down: bfloat16 [32, 704, 2048], P('expert'), may hold values from -0.21875 to 0.21875
- routes: int32 [8, 32, 128, 6], P('dp', 'expert'), may hold values from 0 to 31, all different within a row; in each aligned block of 128 rows (0 to 127, 128 to 255, ..., all dimensions but the last counted through in order) at most 36 rows name the same one
- route_weights: float32 [8, 32, 128, 6], P('dp', 'expert'), may hold values from 0.1 to 0.6
Outputs:
- layer_out: bfloat16 [2048, 16, 2048], P('expert', 'dp')
Inputs may be any that keep to these rules, and one draw needn't show every extreme that they name: `routes`: each row names 6 different experts; within the rows of one device no expert is named more than 36 times.
All inputs are finite; a program needn't handle non-finite values.
Results may differ from a plain program's by a relative error of at most 0.0049.
Values may be sent and summed in bfloat16 or wider, within the bound.
No kernel may reach another device: no remote copies, remote signals or barrier semaphores. Data moves between devices by JAX's collectives and lax.ppermute only.
A program may use at most 128 MiB of HBM per device.

v0:
```python
import jax
import jax.numpy as jnp
from jax import lax
from jax.sharding import PartitionSpec as P

HEADS = 16
NOPE = 128
ROPE = 64
V_DIM = 128
TOP = 6
EPSILON = 1e-06
QUERY_BLOCK = 512


def side_by_side(arrays, axis, split_dim, concat_dim, along):
    widths = [a.shape[along] for a in arrays]
    both = jnp.concatenate(arrays, axis=along)
    result = lax.all_to_all(both, axis, split_axis=split_dim, concat_axis=concat_dim, tiled=True)
    return tuple(jnp.split(result, [sum(widths[:k]) for k in range(1, len(widths))], axis=along))


def feed_forward(rows, gate_matrix, up_matrix, down_matrix):
    gate_part = jnp.dot(rows, gate_matrix, preferred_element_type=jnp.float32)
    up_part = jnp.dot(rows, up_matrix, preferred_element_type=jnp.float32)
    activated = (jax.nn.silu(gate_part) * up_part).astype(jnp.bfloat16)
    return jnp.dot(activated, down_matrix, preferred_element_type=jnp.float32).astype(jnp.bfloat16)


def attend_items(query_items, key_items, value_items, segment_items):
    length, count_items, qk_width = query_items.shape
    block_rows = QUERY_BLOCK
    score_scale = qk_width ** (-0.5)
    key_positions = jnp.arange(length, dtype=jnp.int32)

    def one_block(block_index):
        first_row = block_index * block_rows
        query_block = lax.dynamic_slice_in_dim(query_items, first_row, block_rows, 0)
        scores = (
            jnp.einsum("qid,kid->iqk", query_block, key_items, preferred_element_type=jnp.float32)
            * score_scale
        )
        row_positions = first_row + jnp.arange(block_rows, dtype=jnp.int32)
        row_segments = lax.dynamic_slice_in_dim(segment_items, first_row, block_rows, 1)
        allowed = (row_positions[None, :, None] >= key_positions[None, None, :]) & (
            row_segments[:, :, None] == segment_items[:, None, :]
        )
        scores = jnp.where(allowed, scores, -jnp.inf)
        row_peak = jnp.max(scores, axis=2, keepdims=True)
        raised = jnp.exp(scores - row_peak)
        weights = (raised / jnp.sum(raised, axis=2, keepdims=True)).astype(jnp.bfloat16)
        return jnp.einsum(
            "iqk,kid->qid", weights, value_items, preferred_element_type=jnp.float32
        ).astype(jnp.bfloat16)

    blocks = lax.map(one_block, jnp.arange(length // block_rows, dtype=jnp.int32))
    return blocks.reshape(length, count_items, value_items.shape[2])


def body(
    queries,
    key_nope,
    key_rope,
    values,
    residual,
    segments,
    out_proj,
    norm_gain,
    expert_gate,
    expert_up,
    expert_down,
    routes,
    route_weights,
):
    half_rows, stream_count, query_width = queries.shape
    model_width = residual.shape[2]
    token_rows = half_rows * stream_count
    pair_count = token_rows * TOP
    expert_count = lax.axis_size("expert")
    item_count = stream_count * HEADS // expert_count
    key_heads = jnp.concatenate(
        [
            key_nope.reshape(half_rows, stream_count, HEADS, NOPE),
            jnp.broadcast_to(key_rope[:, :, None, :], (half_rows, stream_count, HEADS, ROPE)),
        ],
        axis=3,
    )
    query_items = queries.reshape(half_rows, stream_count * HEADS, NOPE + ROPE)
    key_items = key_heads.reshape(half_rows, stream_count * HEADS, NOPE + ROPE)
    value_items = values.reshape(half_rows, stream_count * HEADS, V_DIM)
    query_all, key_all, value_all = side_by_side(
        (query_items, key_items, value_items), "expert", 1, 0, 2
    )
    item_ids = lax.axis_index("expert") * item_count + jnp.arange(item_count, dtype=jnp.int32)
    stream_ids = item_ids // HEADS
    selector = (stream_ids[:, None] == jnp.arange(stream_count, dtype=jnp.int32)[None, :]).astype(
        jnp.int32
    )
    segment_items = jnp.sum(selector[:, :, None] * segments[None, :, :], axis=1)
    attended_items = attend_items(query_all, key_all, value_all, segment_items)
    attended_back = lax.all_to_all(
        attended_items, "expert", split_axis=0, concat_axis=1, tiled=True
    )
    attn_rows = attended_back.reshape(token_rows, HEADS * V_DIM)
    projected = jnp.dot(
        attn_rows,
        lax.all_gather(out_proj, ("dp", "expert"), axis=0, tiled=True),
        preferred_element_type=jnp.float32,
    )
    hidden = residual.reshape(token_rows, model_width).astype(jnp.float32) + projected
    mean_square = jnp.mean(hidden * hidden, axis=1, keepdims=True)
    normed = (hidden * lax.rsqrt(mean_square + EPSILON) * norm_gain.astype(jnp.float32)).astype(
        jnp.bfloat16
    )
    capacity = min(token_rows, max(2, token_rows * TOP * 3 // (2 * expert_count)))
    flat_routes = routes.reshape(pair_count)
    matches = (flat_routes[:, None] == jnp.arange(expert_count, dtype=jnp.int32)[None, :]).astype(
        jnp.int32
    )
    earlier = jnp.cumsum(matches, axis=0) - matches
    slot_rank = jnp.sum(earlier * matches, axis=1)
    target = flat_routes * capacity + slot_rank
    pair_ids = jnp.arange(pair_count, dtype=jnp.int32)
    slot_source = (
        jnp.full((expert_count * capacity,), pair_count, jnp.int32).at[target].set(pair_ids)
    )
    slot_live = slot_source < pair_count
    slot_rows = normed[jnp.minimum(slot_source, pair_count - 1) // TOP]
    outgoing = jnp.where(slot_live[:, None], slot_rows, jnp.zeros_like(slot_rows)).reshape(
        expert_count, capacity, model_width
    )
    gate_matrix = expert_gate[0]
    up_matrix = expert_up[0]
    down_matrix = expert_down[0]
    arrived = lax.all_to_all(outgoing, "expert", split_axis=0, concat_axis=0, tiled=True)
    source_count, slot_count, width = arrived.shape
    flat_rows = arrived.reshape(source_count * slot_count, width)
    results = feed_forward(flat_rows, gate_matrix, up_matrix, down_matrix)
    returned = lax.all_to_all(
        results.reshape(source_count, slot_count, width),
        "expert",
        split_axis=0,
        concat_axis=0,
        tiled=True,
    )
    pair_outputs = returned.reshape(expert_count * capacity, model_width)[target]
    weighted = route_weights.reshape(pair_count, 1) * pair_outputs.astype(jnp.float32)
    routed_sum = jnp.sum(weighted.reshape(token_rows, TOP, model_width), axis=1)
    layer_out = (hidden + routed_sum).astype(jnp.bfloat16)
    return layer_out.reshape(half_rows, stream_count, model_width)


def solution(mesh):
    return jax.shard_map(
        body,
        mesh=mesh,
        in_specs=(
            P("expert", "dp", None),
            P("expert", "dp", None),
            P("expert", "dp", None),
            P("expert", "dp", None),
            P("expert", "dp", None),
            P("dp", None),
            P(("dp", "expert"), None),
            P(),
            P("expert", None, None),
            P("expert", None, None),
            P("expert", None, None),
            P("dp", "expert", None, None),
            P("dp", "expert", None, None),
        ),
        out_specs=P("expert", "dp", None),
        check_vma=False,
    )
```

profile of v0, /device:TPU:2, one launch (start us, length us, event | category | flops | bytes accessed | tf_op | source)
XLA Modules:
  0.0 490.3 jit_solution(3616979973672763825)
XLA Ops:
  6.5 0.7 all-gather.2.cloned.1.call-update
  7.3 3.5 reshape.177
  10.8 1.4 concatenate.10
  12.2 2.2 reshape.178
  14.3 0.8 broadcast_in_dim.30
  15.2 2.3 pad_maximum_fusion
  17.5 2.6 copy.45
  20.1 11.7 %all-to-all-start = ((bf16[64,32,512]{2,0,1:T(8,128)(2,1)}), bf16[64,32,512]{2,0,1:T(8,128)(2,1)}, u32[]{:S(2)}, u32[]{:S(2)}) async-start(bf16[64,32,512]{2,0,1:T(8,128)(2,1)} %copy.45), calls=%async_computation | async-start | bytes 4194304 | tf_op jit(solution)/shard_map/all_to_all | solution.py:18
  32.3 1.2 reshape.186
  33.5 1.7 reduce-window.6
  35.3 0.3 slice_reduce_fusion
  35.7 49.4 %all-to-all-done = bf16[64,32,512]{2,0,1:T(8,128)(2,1)} async-done(((bf16[64,32,512]{2,0,1:T(8,128)(2,1)}), bf16[64,32,512]{2,0,1:T(8,128)(2,1)}, u32[]{:S(2)}, u32[]{:S(2)}) %all-to-all-start) | async-done | bytes 2097184 | tf_op jit(solution)/shard_map/all_to_all | solution.py:18
  85.0 1.1 split.14
  86.1 3.6 fusion.27
  89.7 2.2 copy.46
  91.9 2.2 copy.47
  94.1 24.3 %while.11 = (s32[]{:T(128)}, bf16[4,512,1,128]{3,1,2,0:T(8,128)(2,1)}, s32[4]{0:T(128)S(1)}, s32[1,2048]{1,0:T(1,128)S(1)}, bf16[2048,1,192]{0,2,1:T(8,128)(2,1)...) while((s32[]{:T(128)}, ...), condition=%wide.region_4.5_spmd.clone, body=%wide.region_1.4_spmd.clone.sunk | while | flops 682688000 | bytes 14250675 | solution.py:55
  94.1 0.6 dynamic_slice.25
  95.4 2.6 fusion.38
  97.9 0.7 fusion.39
  98.7 1.5 fusion.40
  100.2 0.6 dynamic_slice.25
  101.4 2.6 fusion.38
  104.0 0.7 fusion.39
  104.7 1.5 fusion.40
  106.3 0.6 dynamic_slice.25
  107.5 2.6 fusion.38
  110.1 0.7 fusion.39
  110.8 1.5 fusion.40
  112.3 0.6 dynamic_slice.25
  113.6 2.6 fusion.38
  116.2 0.7 fusion.39
  116.9 1.5 fusion.40
  118.4 0.6 broadcast.129
  119.0 2.1 reduce.10
  121.1 0.9 reshape.220
  122.0 5.5 %all-to-all-start.1 = ((bf16[32,2,4096]{2,1,0:T(2,128)(2,1)}), bf16[32,2,4096]{2,1,0:T(2,128)(2,1)S(1)}, u32[]{:S(2)}, u32[]{:S(2)}) async-start(bf16[32,2,4096]{2,1,0:T(2,128)(2,1)} %reshape.220), calls=%async_computation.1 | async-start | bytes 1048576 | tf_op jit(solution)/shard_map/all_to_all | solution.py:100
  127.5 0.7 copy.51
  128.3 1.0 mul.81
  129.4 3.6 scatter_custom_fusion
  133.1 11.8 %all-to-all-done.1 = bf16[32,2,4096]{2,1,0:T(2,128)(2,1)S(1)} async-done(((bf16[32,2,4096]{2,1,0:T(2,128)(2,1)}), bf16[32,2,4096]{2,1,0:T(2,128)(2,1)S(1)}, u32[]{:S(2)}, u32[]{:S(2)}) %all-to-all-start.1) | async-done | bytes 524320 | tf_op jit(solution)/shard_map/all_to_all | solution.py:100
  144.9 1.8 reshape.221
  146.7 1.3 copy.56
  148.0 1.1 copy.49
  149.2 1.3 reshape.180
  150.5 5.0 %multiply_reduce_fusion.1 = (f32[128]{0:T(128)S(1)}, f32[128,2048]{1,0:T(8,128)S(1)}) fusion(f32[128,2048]{1,0:T(8,128)} %reshape.186, bf16[128,2048]{1,0:T(8,128)(2,1)S(1)} %reshape.180, bf16[2048,2048]{1,0:T(8,128)(2,1)} %all-gather.2.cloned.1.call-done), kind=kOutput, calls=%fused_computation.34 | convolution fusion | flops 1074528128 | bytes 11010560 | tf_op jit(solution)/shard_map/dot_general | solution.py:104
  155.5 1.0 copy-done.1
  156.4 0.2 multiply_convert_fusion
  156.6 6.1 %gather_fusion = bf16[1152,2048]{1,0:T(8,128)(2,1)} fusion(bf16[128,2048]{1,0:T(8,128)(2,1)S(1)} %multiply_convert_fusion, s32[2048]{0:T(1024)S(1)} %pad_clamp_fusion), kind=kCustom, calls=%fused_computation | custom fusion | bytes 9441792 | tf_op jit(solution)/shard_map/gather | solution.py:127
  162.7 7.2 %gather.9 = bf16[32,36,2048]{2,1,0:T(8,128)(2,1)} reshape(bf16[1152,2048]{1,0:T(8,128)(2,1)} %gather_fusion) | data formatting | bytes 9437184 | tf_op jit(solution)/shard_map/gather | solution.py:127
  169.9 2.9 broadcast_select_fusion
  172.8 123.9 %all_to_all.43 = bf16[32,36,2048]{2,1,0:T(8,128)(2,1)} all-to-all(bf16[32,36,2048]{2,1,0:T(8,128)(2,1)S(1)} %broadcast_select_fusion), channel_id=1, replica_groups=mesh['dp'=8,'expert'=32] {'expert'}, dimensions={0} | all-to-all | bytes 9437184 | tf_op jit(solution)/shard_map/all_to_all | solution.py:134
  296.7 7.3 %reshape.182 = bf16[1152,2048]{1,0:T(8,128)(2,1)} reshape(bf16[32,36,2048]{2,1,0:T(8,128)(2,1)} %all_to_all.43) | data formatting | bytes 9437184 | tf_op jit(solution)/shard_map/reshape | solution.py:136
  304.0 7.3 %fusion.16 = f32[1152,704]{0,1:T(8,128)S(1)} fusion(bf16[1152,2048]{1,0:T(8,128)(2,1)} %reshape.182, bf16[1,2048,704]{1,2,0:T(8,128)(2,1)} %param.23), kind=kOutput, calls=%fused_computation.28 | convolution fusion | flops 3321888768 | bytes 10846208 | tf_op jit(solution)/shard_map/dot_general | solution.py:23
  311.3 4.0 fusion.13
  315.4 5.6 %convolution_convert_fusion = bf16[1152,2048]{1,0:T(8,128)(2,1)} fusion(bf16[1152,704]{0,1:T(8,128)(2,1)S(1)} %fusion.13, bf16[1,704,2048]{2,1,0:T(8,128)(2,1)S(1)} %copy-done), kind=kOutput, calls=%fused_computation.22 | convolution fusion | flops 3324248064 | bytes 9224192 | tf_op jit(solution)/shard_map/dot_general | solution.py:26
  320.9 7.3 %reshape.183 = bf16[32,36,2048]{2,1,0:T(8,128)(2,1)} reshape(bf16[1152,2048]{1,0:T(8,128)(2,1)} %convolution_convert_fusion) | data formatting | bytes 9437184 | tf_op jit(solution)/shard_map/reshape | solution.py:139
  328.2 5.4 %all-to-all-start.3 = ((bf16[32,36,2048]{2,1,0:T(8,128)(2,1)}), bf16[32,36,2048]{2,1,0:T(8,128)(2,1)}, u32[]{:S(2)}, u32[]{:S(2)}) async-start(bf16[32,36,2048]{2,1,0:T(8,128)(2,1)} %reshape.183), calls=%async_computation.3 | async-start | bytes 10485760 | tf_op jit(solution)/shard_map/all_to_all | solution.py:138
  333.7 117.9 %all-to-all-done.3 = bf16[32,36,2048]{2,1,0:T(8,128)(2,1)} async-done(((bf16[32,36,2048]{2,1,0:T(8,128)(2,1)}), bf16[32,36,2048]{2,1,0:T(8,128)(2,1)}, u32[]{:S(2)}, u32[]{:S(2)}) %all-to-all-start.3) | async-done | bytes 4718624 | tf_op jit(solution)/shard_map/all_to_all | solution.py:138
  451.6 7.3 %reshape.184 = bf16[1152,2048]{1,0:T(8,128)(2,1)} reshape(bf16[32,36,2048]{2,1,0:T(8,128)(2,1)} %all-to-all-done.3) | data formatting | bytes 9437184 | tf_op jit(solution)/shard_map/reshape | solution.py:145
  458.9 10.0 %gather_fusion.1 = bf16[768,2048]{1,0:T(8,128)(2,1)} fusion(bf16[1152,2048]{1,0:T(8,128)(2,1)} %reshape.184, s32[1024]{0:T(1024)S(1)} %pad_clamp_fusion.1), kind=kCustom, calls=%fused_computation.1 | custom fusion | bytes 6294528 | tf_op jit(solution)/shard_map/gather | solution.py:145
  469.0 6.5 %reshape.187 = f32[128,6,2048]{2,1,0:T(8,128)} reshape(bf16[768,2048]{1,0:T(8,128)(2,1)} %gather_fusion.1) | data formatting | bytes 9437184 | tf_op jit(solution)/shard_map/convert_element_type | solution.py:146
  475.5 6.7 %multiply_reduce_fusion = f32[128,2048]{1,0:T(8,128)S(1)} fusion(f32[128,6,2048]{2,1,0:T(8,128)} %reshape.187, f32[128,6]{1,0:T(8,128)S(1)} %bitcast.100), kind=kLoop, calls=%fused_computation.21 | loop fusion | flops 2883584 | bytes 7343104 | tf_op jit(solution)/shard_map/reduce_sum | solution.py:147
  482.3 1.1 reshape.185
  (51 shorter events, 1.1 us)
Async XLA Ops:
  6.5 308.8 %copy-start = (bf16[1,704,2048]{2,1,0:T(8,128)(2,1)S(1)}, bf16[1,704,2048]{2,1,0:T(8,128)(2,1)}, u32[]{:S(2)}) copy-start(bf16[1,704,2048]{2,1,0:T(8,128)(2,1)} %param.25) | copy-start | bytes 8650756
  6.5 143.9 %all-gather.2.cloned.1.call-start = ((), (), s32[]{:S(2)}) async-start(), calls=%async_computation.4 | async-start | bytes 8421376 | tf_op jit(solution)/shard_map/all_gather | solution.py:106
  17.5 14.4 %copy-start.6 = (s32[1,1,128,6]{2,1,3,0:T(1,128)S(1)}, s32[1,1,128,6]{2,1,3,0:T(1,128)}, u32[]{:S(2)}) copy-start(s32[1,1,128,6]{2,1,3,0:T(1,128)} %param.26) | copy-start | bytes 9220
  17.5 14.8 %copy-start.4 = (bf16[64,2,2048]{2,1,0:T(2,128)(2,1)S(1)}, bf16[64,2,2048]{2,1,0:T(2,128)(2,1)}, u32[]{:S(2)}) copy-start(bf16[64,2,2048]{2,1,0:T(2,128)(2,1)} %param.19) | copy-start | bytes 1572868
  17.5 16.0 %copy-start.7 = (bf16[2048]{0:T(1024)(128)(2,1)S(1)}, bf16[2048]{0:T(1024)(128)(2,1)}, u32[]{:S(2)}) copy-start(bf16[2048]{0:T(1024)(128)(2,1)} %param.22) | copy-start | bytes 12292
  20.1 15.5 %copy-start.5 = (s32[2,2048]{1,0:T(2,128)S(1)}, s32[2,2048]{1,0:T(2,128)}, u32[]{:S(2)}) copy-start(s32[2,2048]{1,0:T(2,128)} %param.20) | copy-start | bytes 49156
  20.1 64.9 %all-to-all-start = ((bf16[64,32,512]{2,0,1:T(8,128)(2,1)}), bf16[64,32,512]{2,0,1:T(8,128)(2,1)}, u32[]{:S(2)}, u32[]{:S(2)}) async-start(bf16[64,32,512]{2,0,1:T(8,128)(2,1)} %copy.45), calls=%async_computation | async-start | bytes 4194304 | tf_op jit(solution)/shard_map/all_to_all | solution.py:18
  122.0 22.9 %all-to-all-start.1 = ((bf16[32,2,4096]{2,1,0:T(2,128)(2,1)}), bf16[32,2,4096]{2,1,0:T(2,128)(2,1)S(1)}, u32[]{:S(2)}, u32[]{:S(2)}) async-start(bf16[32,2,4096]{2,1,0:T(2,128)(2,1)} %reshape.220), calls=%async_computation.1 | async-start | bytes 1048576 | tf_op jit(solution)/shard_map/all_to_all | solution.py:100
  155.4 1.0 copy-start.1
  304.0 7.3 %copy-start.3 = (bf16[1152,2048]{1,0:T(8,128)(2,1)S(1)}, bf16[1152,2048]{1,0:T(8,128)(2,1)}, u32[]{:S(2)}) copy-start(bf16[1152,2048]{1,0:T(8,128)(2,1)} %reshape.182) | copy-start | bytes 14155780
  304.0 7.3 %copy-start.9 = (bf16[1,2048,704]{1,2,0:T(8,128)(2,1)S(1)}, bf16[1,2048,704]{1,2,0:T(8,128)(2,1)}, u32[]{:S(2)}) copy-start(bf16[1,2048,704]{1,2,0:T(8,128)(2,1)} %param.24) | copy-start | bytes 8650756
  328.2 5.4 %copy-start.8 = (f32[1,1,128,6]{2,1,3,0:T(1,128)S(1)}, f32[1,1,128,6]{2,1,3,0:T(1,128)}, u32[]{:S(2)}) copy-start(f32[1,1,128,6]{2,1,3,0:T(1,128)} %param.27) | copy-start | bytes 9220
  328.2 123.4 %all-to-all-start.3 = ((bf16[32,36,2048]{2,1,0:T(8,128)(2,1)}), bf16[32,36,2048]{2,1,0:T(8,128)(2,1)}, u32[]{:S(2)}, u32[]{:S(2)}) async-start(bf16[32,36,2048]{2,1,0:T(8,128)(2,1)} %reshape.183), calls=%async_computation.3 | async-start | bytes 10485760 | tf_op jit(solution)/shard_map/all_to_all | solution.py:138
  475.5 6.7 %copy-start.2 = (f32[128,2048]{1,0:T(8,128)S(1)}, f32[128,2048]{1,0:T(8,128)}, u32[]{:S(2)}) copy-start(f32[128,2048]{1,0:T(8,128)} %copy-done.1) | copy-start | bytes 3145732
Sparse Core Ops, SparseCore 0:
  11.0 128.0 all-gather.1
where the time goes:
time: 492 us; the launch traced here: 490 us
  waiting for transfers between devices  180 us (37%)
  blocking collectives  124 us (25%)
  local copies, waits for them, and re-layouts  90.1 us (18%)
  matrix products  38.3 us (8%)
  starting transfers between devices  22.7 us (5%)
  other arithmetic  19.1 us (4%)
  between operations  13.7 us (3%)
    all_to_all x1, blocking collectives, body(): lax.all_to_all(outgoing, 'expert', split_axis=0, concat_axis=0, tiled=True)  124 us
    all_to_all x1, waiting for transfers between devices, body(): lax.all_to_all(results.reshape(source_count, slot_count, width), 'expert'...  118 us
    all_to_all x1, waiting for transfers between devices, side_by_side(): lax.all_to_all(both, axis, split_axis=split_dim, concat_axis=concat_dim,...  49.4 us
    gather x2, local copies, waits for them, and re-layouts, body(): slot_rows = normed[jnp.minimum(slot_source, pair_count - 1) // TOP]  13.3 us
    all_to_all x1, waiting for transfers between devices, body(): lax.all_to_all(attended_items, 'expert', split_axis=0, concat_axis=1, til...  11.8 us
    all_to_all x1, starting transfers between devices, side_by_side(): lax.all_to_all(both, axis, split_axis=split_dim, concat_axis=concat_dim,...  11.7 us
    dot_general x4, matrix products, one_block(): jnp.einsum('qid,kid->iqk', query_block, key_items, preferred_element_type...  10.3 us
    gather x1, local copies, waits for them, and re-layouts, body(): returned.reshape(expert_count * capacity, model_width)[target]  10 us
  transfers between devices with their start and end apart: 4, of which 3 were waited for; matrix products, arithmetic and copies ran while one was open for 13% of the time, Pallas kernels for 0%

commit v1 on v0

--- a/solution.py
+++ b/solution.py
@@ -97,9 +97,10 @@
     )
     segment_items = jnp.sum(selector[:, :, None] * segments[None, :, :], axis=1)
     attended_items = attend_items(query_all, key_all, value_all, segment_items)
-    attended_back = lax.all_to_all(
-        attended_items, "expert", split_axis=0, concat_axis=1, tiled=True
-    )
+    size = lax.axis_size("expert")
+    shards = jnp.stack(jnp.split(attended_items, size, axis=0), axis=0)
+    shards = lax.all_to_all(shards, "expert", split_axis=0, concat_axis=0)
+    attended_back = jnp.concatenate(shards, axis=1)
     attn_rows = attended_back.reshape(token_rows, HEADS * V_DIM)
     projected = jnp.dot(
         attn_rows,

time: 492 us -> 506 us (1.028)
  local copies, waits for them, and re-layouts: 90.1 us -> 107 us
    unnamed x26 -> x56, local copies, waits for them, and re-layouts: 9.58 us -> 24.4 us
  transfers between devices with their start and end apart: 4 -> 4, of which waited for: 3 -> 3; matrix products, arithmetic and copies ran while one was open for 13% -> 12% of each run, Pallas kernels for 0% -> 0%
where the time goes in v1:
time: 506 us; the launch traced here: 503 us
  waiting for transfers between devices  180 us (36%)
  blocking collectives  124 us (25%)
  local copies, waits for them, and re-layouts  107 us (21%)
  matrix products  35.9 us (7%)
  starting transfers between devices  23.3 us (5%)
  other arithmetic  17 us (3%)
  between operations  13.8 us (3%)
    all_to_all x1, blocking collectives, body(): lax.all_to_all(outgoing, 'expert', split_axis=0, concat_axis=0, tiled=True)  124 us
    all_to_all x1, waiting for transfers between devices, body(): lax.all_to_all(results.reshape(source_count, slot_count, width), 'expert'...  118 us
    all_to_all x1, waiting for transfers between devices, side_by_side(): lax.all_to_all(both, axis, split_axis=split_dim, concat_axis=concat_dim,...  46.2 us
    unnamed x56, local copies, waits for them, and re-layouts  24.4 us
    all_to_all x1, waiting for transfers between devices, body(): shards = lax.all_to_all(shards, 'expert', split_axis=0, concat_axis=0)  15 us
    gather x2, local copies, waits for them, and re-layouts, body(): slot_rows = normed[jnp.minimum(slot_source, pair_count - 1) // TOP]  13.2 us
    all_to_all x1, starting transfers between devices, side_by_side(): lax.all_to_all(both, axis, split_axis=split_dim, concat_axis=concat_dim,...  11.7 us
    dot_general x4, matrix products, one_block(): jnp.einsum('qid,kid->iqk', query_block, key_items, preferred_element_type...  10.3 us
  transfers between devices with their start and end apart: 4, of which 3 were waited for; matrix products, arithmetic and copies ran while one was open for 12% of the time, Pallas kernels for 0%

profile of v1, /device:TPU:2, one launch (start us, length us, event | category | flops | bytes accessed | tf_op | source)
XLA Modules:
  0.0 503.4 jit_solution(4057200673317772792)
XLA Ops:
  6.5 3.5 reshape.176
  10.0 1.4 concatenate.10
  11.4 2.2 reshape.177
  13.6 0.8 broadcast_in_dim.30
  14.4 2.3 pad_maximum_fusion
  16.8 2.5 copy.67
  19.2 11.7 %all-to-all-start = ((bf16[64,32,512]{2,0,1:T(8,128)(2,1)}), bf16[64,32,512]{2,0,1:T(8,128)(2,1)}, u32[]{:S(2)}, u32[]{:S(2)}) async-start(bf16[64,32,512]{2,0,1:T(8,128)(2,1)} %copy.67), calls=%async_computation | async-start | bytes 4194304 | tf_op jit(solution)/shard_map/all_to_all | solution.py:18
  31.0 0.7 all-gather.2.cloned.1.call-update
  32.1 1.2 reshape.185
  33.4 1.7 reduce-window.6
  35.5 46.2 %all-to-all-done = bf16[64,32,512]{2,0,1:T(8,128)(2,1)} async-done(((bf16[64,32,512]{2,0,1:T(8,128)(2,1)}), bf16[64,32,512]{2,0,1:T(8,128)(2,1)}, u32[]{:S(2)}, u32[]{:S(2)}) %all-to-all-start) | async-done | bytes 2097184 | tf_op jit(solution)/shard_map/all_to_all | solution.py:18
  81.8 1.9 split.142
  83.6 3.5 fusion.27
  87.1 2.3 copy.68
  89.4 2.2 copy.69
  91.6 23.3 %while.11 = (s32[]{:T(128)}, bf16[4,512,1,128]{3,1,2,0:T(8,128)(2,1)S(1)}, s32[4]{0:T(128)S(1)}, s32[1,2048]{1,0:T(1,128)S(1)}, bf16[2048,1,192]{0,2,1:T(8,128)(...) while((s32[]{:T(128)}, ...), condition=%wide.region_4.5_spmd.clone, body=%wide.region_1.4_spmd.clone.sunk | while | flops 682688000 | bytes 16347347 | solution.py:55
  92.8 2.6 fusion.38
  95.5 0.7 fusion.39
  96.5 0.9 fusion.40
  98.7 2.6 fusion.38
  101.3 0.7 fusion.39
  102.3 0.9 fusion.40
  104.5 2.6 fusion.38
  107.1 0.7 fusion.39
  108.2 0.9 fusion.40
  110.4 2.6 fusion.38
  113.0 0.7 fusion.39
  114.0 0.9 fusion.40
  114.9 0.6 constant_dynamic-update-slice_fusion.31
  115.5 0.6 constant_dynamic-update-slice_fusion.30
  116.1 0.6 constant_dynamic-update-slice_fusion.29
  116.8 0.6 constant_dynamic-update-slice_fusion.28
  117.4 0.6 constant_dynamic-update-slice_fusion.27
  119.2 0.6 constant_dynamic-update-slice_fusion.24
  119.8 0.6 constant_dynamic-update-slice_fusion.23
  120.4 0.6 constant_dynamic-update-slice_fusion.22
  121.0 0.6 constant_dynamic-update-slice_fusion.21
  121.6 0.6 constant_dynamic-update-slice_fusion.20
  122.2 0.6 constant_dynamic-update-slice_fusion.19
  134.4 6.1 %all-to-all-start.1 = ((bf16[32,64,1,128]{3,1,2,0:T(8,128)(2,1)}), bf16[32,64,1,128]{3,1,2,0:T(8,128)(2,1)S(1)}, u32[]{:S(2)}, u32[]{:S(2)}) async-start(bf16[32,64,1,128]{3,1,2,0:T(8,128)(2,1)} %constant_dynamic-update-slice_fusion), calls=%async_computation.1 | async-start | bytes 1048576 | tf_op jit(solution)/shard_map/all_to_all | solution.py:102
  140.4 0.7 copy.72
  141.2 1.0 mul.81
  142.3 3.6 scatter_custom_fusion
  146.0 15.0 %all-to-all-done.1 = bf16[32,64,1,128]{3,1,2,0:T(8,128)(2,1)S(1)} async-done(((bf16[32,64,1,128]{3,1,2,0:T(8,128)(2,1)}), bf16[32,64,1,128]{3,1,2,0:T(8,128)(2,1)S(1)}, u32[]{:S(2)}, u32[]{:S(2)}) %all-to-all-start.1) | async-done | bytes 524320 | tf_op jit(solution)/shard_map/all_to_all | solution.py:102
  161.0 1.1 copy.70
  162.2 1.3 reshape_reshape.3
  163.5 5.0 multiply_reduce_fusion.1
  168.5 1.0 copy-done.1
  169.6 6.0 %gather_fusion = bf16[1152,2048]{1,0:T(8,128)(2,1)} fusion(bf16[128,2048]{1,0:T(8,128)(2,1)S(1)} %multiply_convert_fusion, s32[2048]{0:T(1024)S(1)} %pad_clamp_fusion), kind=kCustom, calls=%fused_computation | custom fusion | bytes 9441792 | tf_op jit(solution)/shard_map/gather | solution.py:128
  175.6 7.2 %gather.9 = bf16[32,36,2048]{2,1,0:T(8,128)(2,1)} reshape(bf16[1152,2048]{1,0:T(8,128)(2,1)} %gather_fusion) | data formatting | bytes 9437184 | tf_op jit(solution)/shard_map/gather | solution.py:128
  182.8 2.9 broadcast_select_fusion
  185.7 124.3 %all_to_all.33 = bf16[32,36,2048]{2,1,0:T(8,128)(2,1)} all-to-all(bf16[32,36,2048]{2,1,0:T(8,128)(2,1)S(1)} %broadcast_select_fusion), channel_id=1, replica_groups=mesh['dp'=8,'expert'=32] {'expert'}, dimensions={0} | all-to-all | bytes 9437184 | tf_op jit(solution)/shard_map/all_to_all | solution.py:135
  310.0 7.2 %reshape.181 = bf16[1152,2048]{1,0:T(8,128)(2,1)} reshape(bf16[32,36,2048]{2,1,0:T(8,128)(2,1)} %all_to_all.33) | data formatting | bytes 9437184 | tf_op jit(solution)/shard_map/reshape | solution.py:137
  317.2 7.3 %fusion.16 = f32[1152,704]{0,1:T(8,128)S(1)} fusion(bf16[1152,2048]{1,0:T(8,128)(2,1)} %reshape.181, bf16[1,2048,704]{1,2,0:T(8,128)(2,1)} %param.23), kind=kOutput, calls=%fused_computation.28 | convolution fusion | flops 3321888768 | bytes 10846208 | tf_op jit(solution)/shard_map/dot_general | solution.py:23
  324.5 4.0 fusion.13
  328.5 5.6 %convolution_convert_fusion = bf16[1152,2048]{1,0:T(8,128)(2,1)} fusion(bf16[1152,704]{0,1:T(8,128)(2,1)S(1)} %fusion.13, bf16[1,704,2048]{2,1,0:T(8,128)(2,1)S(1)} %copy-done), kind=kOutput, calls=%fused_computation.22 | convolution fusion | flops 3324248064 | bytes 9224192 | tf_op jit(solution)/shard_map/dot_general | solution.py:26
  334.1 7.2 %reshape.182 = bf16[32,36,2048]{2,1,0:T(8,128)(2,1)} reshape(bf16[1152,2048]{1,0:T(8,128)(2,1)} %convolution_convert_fusion) | data formatting | bytes 9437184 | tf_op jit(solution)/shard_map/reshape | solution.py:140
  341.3 5.4 %all-to-all-start.3 = ((bf16[32,36,2048]{2,1,0:T(8,128)(2,1)}), bf16[32,36,2048]{2,1,0:T(8,128)(2,1)}, u32[]{:S(2)}, u32[]{:S(2)}) async-start(bf16[32,36,2048]{2,1,0:T(8,128)(2,1)} %reshape.182), calls=%async_computation.3 | async-start | bytes 10485760 | tf_op jit(solution)/shard_map/all_to_all | solution.py:139
  346.9 117.9 %all-to-all-done.3 = bf16[32,36,2048]{2,1,0:T(8,128)(2,1)} async-done(((bf16[32,36,2048]{2,1,0:T(8,128)(2,1)}), bf16[32,36,2048]{2,1,0:T(8,128)(2,1)}, u32[]{:S(2)}, u32[]{:S(2)}) %all-to-all-start.3) | async-done | bytes 4718624 | tf_op jit(solution)/shard_map/all_to_all | solution.py:139
  464.7 7.2 %reshape.183 = bf16[1152,2048]{1,0:T(8,128)(2,1)} reshape(bf16[32,36,2048]{2,1,0:T(8,128)(2,1)} %all-to-all-done.3) | data formatting | bytes 9437184 | tf_op jit(solution)/shard_map/reshape | solution.py:146
  471.9 10.1 %gather_fusion.1 = bf16[768,2048]{1,0:T(8,128)(2,1)} fusion(bf16[1152,2048]{1,0:T(8,128)(2,1)} %reshape.183, s32[1024]{0:T(1024)S(1)} %pad_clamp_fusion.1), kind=kCustom, calls=%fused_computation.1 | custom fusion | bytes 6294528 | tf_op jit(solution)/shard_map/gather | solution.py:146
  482.0 6.6 %reshape.186 = f32[128,6,2048]{2,1,0:T(8,128)} reshape(bf16[768,2048]{1,0:T(8,128)(2,1)} %gather_fusion.1) | data formatting | bytes 9437184 | tf_op jit(solution)/shard_map/convert_element_type | solution.py:147
  488.6 6.7 %multiply_reduce_fusion = f32[128,2048]{1,0:T(8,128)S(1)} fusion(f32[128,6,2048]{2,1,0:T(8,128)} %reshape.186, f32[128,6]{1,0:T(8,128)S(1)} %bitcast.258), kind=kLoop, calls=%fused_computation.21 | loop fusion | flops 2883584 | bytes 7343104 | tf_op jit(solution)/shard_map/reduce_sum | solution.py:148
  495.4 1.1 reshape.184
  (88 shorter events, 18.0 us)
Async XLA Ops:
  6.5 322.0 %copy-start = (bf16[1,704,2048]{2,1,0:T(8,128)(2,1)S(1)}, bf16[1,704,2048]{2,1,0:T(8,128)(2,1)}, u32[]{:S(2)}) copy-start(bf16[1,704,2048]{2,1,0:T(8,128)(2,1)} %param.25) | copy-start | bytes 8650756
  16.7 15.0 %copy-start.8 = (s32[1,1,128,6]{2,1,3,0:T(1,128)S(1)}, s32[1,1,128,6]{2,1,3,0:T(1,128)}, u32[]{:S(2)}) copy-start(s32[1,1,128,6]{2,1,3,0:T(1,128)} %param.26) | copy-start | bytes 9220
  16.7 15.4 %copy-start.4 = (bf16[64,2,2048]{2,1,0:T(2,128)(2,1)S(1)}, bf16[64,2,2048]{2,1,0:T(2,128)(2,1)}, u32[]{:S(2)}) copy-start(bf16[64,2,2048]{2,1,0:T(2,128)(2,1)} %param.19) | copy-start | bytes 1572868
  16.7 16.6 %copy-start.9 = (bf16[2048]{0:T(1024)(128)(2,1)S(1)}, bf16[2048]{0:T(1024)(128)(2,1)}, u32[]{:S(2)}) copy-start(bf16[2048]{0:T(1024)(128)(2,1)} %param.22) | copy-start | bytes 12292
  19.2 16.2 %copy-start.7 = (s32[2,2048]{1,0:T(2,128)S(1)}, s32[2,2048]{1,0:T(2,128)}, u32[]{:S(2)}) copy-start(s32[2,2048]{1,0:T(2,128)} %param.20) | copy-start | bytes 49156
  19.2 62.5 %all-to-all-start = ((bf16[64,32,512]{2,0,1:T(8,128)(2,1)}), bf16[64,32,512]{2,0,1:T(8,128)(2,1)}, u32[]{:S(2)}, u32[]{:S(2)}) async-start(bf16[64,32,512]{2,0,1:T(8,128)(2,1)} %copy.67), calls=%async_computation | async-start | bytes 4194304 | tf_op jit(solution)/shard_map/all_to_all | solution.py:18
  31.0 132.5 %all-gather.2.cloned.1.call-start = ((), (), s32[]{:S(2)}) async-start(), calls=%async_computation.4 | async-start | bytes 8421376 | tf_op jit(solution)/shard_map/all_gather | solution.py:107
  83.6 8.0 %copy-start.5 = (bf16[4,512,1,128]{3,1,2,0:T(8,128)(2,1)S(1)}, bf16[4,512,1,128]{3,1,2,0:T(8,128)(2,1)}, u32[]{:S(2)}) copy-start(bf16[4,512,1,128]{3,1,2,0:T(8,128)(2,1)} %custom-call.5) | copy-start | bytes 1572868
  95.5 1.0 copy-start.6
  101.3 1.1 copy-start.6
  107.1 1.0 copy-start.6
  113.0 1.0 copy-start.6
  134.4 26.7 %all-to-all-start.1 = ((bf16[32,64,1,128]{3,1,2,0:T(8,128)(2,1)}), bf16[32,64,1,128]{3,1,2,0:T(8,128)(2,1)S(1)}, u32[]{:S(2)}, u32[]{:S(2)}) async-start(bf16[32,64,1,128]{3,1,2,0:T(8,128)(2,1)} %constant_dynamic-update-slice_fusion), calls=%async_computation.1 | async-start | bytes 1048576 | tf_op jit(solution)/shard_map/all_to_all | solution.py:102
  168.5 1.0 copy-start.1
  317.2 7.3 %copy-start.3 = (bf16[1152,2048]{1,0:T(8,128)(2,1)S(1)}, bf16[1152,2048]{1,0:T(8,128)(2,1)}, u32[]{:S(2)}) copy-start(bf16[1152,2048]{1,0:T(8,128)(2,1)} %reshape.181) | copy-start | bytes 14155780
  317.2 7.3 %copy-start.11 = (bf16[1,2048,704]{1,2,0:T(8,128)(2,1)S(1)}, bf16[1,2048,704]{1,2,0:T(8,128)(2,1)}, u32[]{:S(2)}) copy-start(bf16[1,2048,704]{1,2,0:T(8,128)(2,1)} %param.24) | copy-start | bytes 8650756
  341.3 5.4 %copy-start.10 = (f32[1,1,128,6]{2,1,3,0:T(1,128)S(1)}, f32[1,1,128,6]{2,1,3,0:T(1,128)}, u32[]{:S(2)}) copy-start(f32[1,1,128,6]{2,1,3,0:T(1,128)} %param.27) | copy-start | bytes 9220
  341.3 123.4 %all-to-all-start.3 = ((bf16[32,36,2048]{2,1,0:T(8,128)(2,1)}), bf16[32,36,2048]{2,1,0:T(8,128)(2,1)}, u32[]{:S(2)}, u32[]{:S(2)}) async-start(bf16[32,36,2048]{2,1,0:T(8,128)(2,1)} %reshape.182), calls=%async_computation.3 | async-start | bytes 10485760 | tf_op jit(solution)/shard_map/all_to_all | solution.py:139
  488.6 6.7 %copy-start.2 = (f32[128,2048]{1,0:T(8,128)S(1)}, f32[128,2048]{1,0:T(8,128)}, u32[]{:S(2)}) copy-start(f32[128,2048]{1,0:T(8,128)} %copy-done.1) | copy-start | bytes 3145732
Sparse Core Ops, SparseCore 0:
  35.5 127.1 all-gather.1
